TPU v7x, 32 devices: a whole 2x2x4 slice. The times are simulated.
32 devices in a mesh: beam: 2 (over x), tm: 16 (over z, y, core).
Axes of the slice: x: 2, y: 2, z: 4, core: 2. Of those that a mesh axis runs over, the one named last changes fastest.
Arguments:
- voltage: bfloat16 [2, 2, 2097152], P(None, None, ('beam', 'tm')), parts along dimension 2, may hold values from -11 to 11
- delays: int32 [64, 2048], replicated, may hold values from 0 to 96, as said below
- chan_mask: int32 [4096], P('beam'), parts along dimension 0, may hold values 0 or 1
Outputs:
- zscore: float32 [64, 1024], P(None, ('beam', 'tm')), parts along dimension 1
- trial_stats: float32 [3, 128], P(None, 'beam'), parts along dimension 1
There are 2 independent parts, one for each index of `beam`. A program takes and returns all parts, laid end to end along the dimension named above; an argument that names none is the same for every part. Nothing has to cross between parts.
Inputs may be any that keep to these rules, and one draw needn't show every extreme that they name: For each trial the delays never rise from one channel to the next; the last channel's delays are 0, and the first channel's delay of some trial is 96.
All inputs are finite; a program needn't handle non-finite values.
Results may differ from a plain program's by a relative error of at most 0.002.
Values may be sent and summed in bfloat16 or wider, within the bound.
No kernel may reach another device: no remote copies, remote signals or barrier semaphores. Data moves between devices by JAX's collectives and lax.ppermute only.
A program may use at most 64 MiB of HBM per device.

v0:
```python
import math
import jax
import jax.numpy as jnp
from jax import lax
from jax.sharding import PartitionSpec as P

NCHAN = 2048
TAPS = 16
DSPAN = 3
highest = lax.Precision.HIGHEST
shift_group = 8


def passed_along(value, axis, steps):
    count = lax.axis_size(axis)
    first, last = (max(0, -steps), min(count, count - steps))
    return lax.ppermute(value, axis, [(source, source + steps) for source in range(first, last)])


def prototype(tap_count, chan_count):
    length = tap_count * chan_count
    position = jnp.arange(length, dtype=jnp.float32)
    centred = (position - (length - 1) / 2.0) / chan_count
    window = 0.54 - 0.46 * jnp.cos(2.0 * jnp.pi * position / (length - 1))
    shaped = jnp.sinc(centred) * window
    shaped = shaped * jnp.sqrt(chan_count / jnp.sum(shaped * shaped))
    return shaped.reshape(tap_count, chan_count)


def phase_table(row_count, col_count, period):
    product = (
        jnp.arange(row_count, dtype=jnp.int32)[:, None]
        * jnp.arange(col_count, dtype=jnp.int32)[None, :]
        % period
    )
    angles = product.astype(jnp.float32) * (-2.0 * jnp.pi / period)
    return (jnp.cos(angles), jnp.sin(angles))


def spectral_power(weighted, chan_count):
    frame_count = weighted.shape[2]
    low_count = chan_count // 128
    split_up = weighted.reshape(2, 2, frame_count, low_count, 128)
    real_part = split_up[:, 0]
    imag_part = split_up[:, 1]
    cos_first, sin_first = phase_table(low_count, low_count, low_count)
    section_real = jnp.einsum(
        "pfmn,mk->pfkn", real_part, cos_first, precision=highest
    ) - jnp.einsum("pfmn,mk->pfkn", imag_part, sin_first, precision=highest)
    section_imag = jnp.einsum(
        "pfmn,mk->pfkn", real_part, sin_first, precision=highest
    ) + jnp.einsum("pfmn,mk->pfkn", imag_part, cos_first, precision=highest)
    cos_twist, sin_twist = phase_table(low_count, 128, chan_count)
    twist_real = section_real * cos_twist - section_imag * sin_twist
    twist_imag = section_real * sin_twist + section_imag * cos_twist
    cos_second, sin_second = phase_table(128, 128, 128)
    scale_factor = 1.0 / math.sqrt(chan_count)
    cos_second = cos_second * scale_factor
    sin_second = sin_second * scale_factor
    final_real = jnp.einsum(
        "pfkn,nj->pfkj", twist_real, cos_second, precision=highest
    ) - jnp.einsum("pfkn,nj->pfkj", twist_imag, sin_second, precision=highest)
    final_imag = jnp.einsum(
        "pfkn,nj->pfkj", twist_real, sin_second, precision=highest
    ) + jnp.einsum("pfkn,nj->pfkj", twist_imag, cos_second, precision=highest)
    energy = jnp.sum(final_real * final_real + final_imag * final_imag, axis=0)
    return jnp.transpose(energy, (2, 1, 0)).reshape(chan_count, frame_count).astype(jnp.bfloat16)


def dedisperse(padded, delays, out_width, max_delay):
    chan_count = padded.shape[0]
    group_count = (max_delay + shift_group) // shift_group
    needed = out_width + group_count * shift_group
    padded = jnp.concatenate(
        [padded, jnp.zeros((chan_count, needed - padded.shape[1]), padded.dtype)], axis=1
    )
    within = jnp.arange(shift_group, dtype=jnp.int32)

    def add_group(group_index, running):
        base = (group_index * shift_group).astype(jnp.int32)
        window = lax.dynamic_slice_in_dim(padded, base, out_width + shift_group - 1, 1)
        stacked = jnp.stack(
            [window[:, offset : offset + out_width] for offset in range(shift_group)]
        )
        targets = base + within
        selector = (delays[:, None, :] == targets[None, :, None]).astype(jnp.bfloat16)
        return running + jnp.einsum(
            "dsk,skt->dt", selector, stacked, preferred_element_type=jnp.float32
        )

    zero_sums = jnp.zeros((delays.shape[0], out_width), jnp.float32)
    return lax.fori_loop(0, group_count, add_group, zero_sums)


def per_device(voltage, delays, chan_mask):
    frame_count = voltage.shape[2] // NCHAN
    framed = voltage.reshape(2, 2, frame_count, NCHAN)
    history = passed_along(framed[:, :, frame_count - (TAPS - 1) :], "tm", 1)
    extended = jnp.concatenate([history, framed], axis=2)
    coeffs = prototype(TAPS, NCHAN)
    weighted = jnp.zeros((2, 2, frame_count, NCHAN), jnp.float32)
    for tap_index in range(TAPS):
        weighted = weighted + coeffs[tap_index] * extended[
            :, :, tap_index : tap_index + frame_count
        ].astype(jnp.float32)
    detected = spectral_power(weighted, NCHAN)
    masked = detected * chan_mask.astype(jnp.bfloat16)[:, None]
    max_delay = DSPAN * frame_count
    gathered = masked
    held_shards = 1
    while held_shards < DSPAN + 1:
        fetched = passed_along(gathered, "tm", -held_shards)
        gathered = jnp.concatenate([gathered, fetched], axis=1)
        held_shards = held_shards * 2
    series = dedisperse(gathered, delays, frame_count, max_delay)
    local_frames = series.shape[1]
    total_frames = local_frames * lax.axis_size("tm")
    totals = lax.psum(jnp.sum(series, axis=1), "tm")
    peak_value = lax.pmax(jnp.max(series, axis=1), "tm")
    average = totals / total_frames
    centred = series - average[:, None]
    variance = lax.psum(jnp.sum(centred * centred, axis=1), "tm") / total_frames
    deviation = jnp.sqrt(variance + 1e-05)
    zscore = centred / deviation[:, None]
    live_count = jnp.maximum(jnp.sum(chan_mask).astype(jnp.float32), 1.0)
    trial_stats = jnp.stack(
        [average / live_count, deviation / live_count, (peak_value - average) / deviation]
    )
    return (zscore, trial_stats)


def solution(mesh):
    in_specs = (P(None, None, ("beam", "tm")), P(), P("beam"))
    out_specs = (P(None, ("beam", "tm")), P(None, "beam"))
    return jax.shard_map(
        per_device, mesh=mesh, in_specs=in_specs, out_specs=out_specs, check_vma=False
    )
```

profile of v0, /device:TPU:0, one launch (start us, length us, event | category | flops | bytes accessed | tf_op | source)
XLA Modules:
  0.0 158.4 jit_solution(6258443623836400769)
XLA Ops:
  0.6 1.4 reshape.106
  2.0 0.0 copy-start
  2.1 0.1 slice.217
  2.2 2.4 %collective-permute-start = (bf16[2,2,15,2048]{3,2,0,1:T(8,128)(2,1)S(1)}, bf16[2,2,15,2048]{3,2,0,1:T(8,128)(2,1)S(1)}, u32[]{:S(2)}, u32[]{:S(2)}) collective-permute-start(bf16[2,2,15,2048]{3,2,0,1:T(8,128)(2,1)S(1)} %slice.217), channel_id=1, source_target_pairs={{0,1},{1,2},{2,3},{3,4},{4,5},{5,6},{6,7},{7,8},{8,9},{9,10},{10,1... | collective-permute-start | bytes 737288 | tf_op jit(solution)/shard_map/ppermute | solution.py:17
  4.6 1.2 multiply_reduce_fusion
  6.6 0.6 broadcast_multiply_fusion
  7.2 0.6 fusion.155
  7.8 0.1 fusion.108
  7.9 2.6 %multiply_add_fusion = f32[2,2,32,2048]{3,2,0,1:T(8,128)S(1)} fusion(bf16[2,2,32,2048]{3,2,0,1:T(8,128)(2,1)S(1)} %copy.12, bf16[2,2,15,2048]{3,2,0,1:T(8,128)(2,1)S(1)} %collective-permute-done, f32[2048]{0:T(1024)S(1)} %get-tuple-element.133, f32[2048]{0:T(1024)S(1)} %get-tuple-element.134, f32[2048]{0:T(1024)S(1)} %get-tuple-element.135, ...), kind=kLoop, calls=%fused_computation.61 | loop fusion | flops 24117248 | bytes 1949696 | tf_op jit(solution)/shard_map/add | solution.py:103
  10.6 0.2 copy.21
  10.8 0.6 fusion.45
  11.4 0.6 fusion.44
  12.0 0.6 convolution_subtract_fusion.1
  12.6 0.6 convolution_add_fusion.1
  13.2 0.8 fusion.40
  14.1 0.8 fusion.42
  14.9 0.8 fusion.22
  15.7 0.8 fusion.23
  16.6 0.5 copy.15
  17.1 0.3 bitcast_multiply_fusion
  17.4 1.3 collective-permute-start.1
  18.7 4.6 %collective-permute-done.1 = bf16[2048,32]{1,0:T(8,128)(2,1)S(1)} collective-permute-done((bf16[2048,32]{1,0:T(8,128)(2,1)S(1)}, bf16[2048,32]{1,0:T(8,128)(2,1)S(1)}, u32[]{:S(2)}, u32[]{:S(2)}) %collective-permute-start.1) | collective-permute-done | bytes 131104 | tf_op jit(solution)/shard_map/ppermute | solution.py:17
  23.3 0.3 pad_maximum_fusion.1
  23.6 1.5 collective-permute-start.2
  25.8 18.1 %collective-permute-done.2 = bf16[2048,64]{1,0:T(8,128)(2,1)S(1)} collective-permute-done((bf16[2048,64]{1,0:T(8,128)(2,1)S(1)}, bf16[2048,64]{1,0:T(8,128)(2,1)S(1)}, u32[]{:S(2)}, u32[]{:S(2)}) %collective-permute-start.2) | collective-permute-done | bytes 262176 | tf_op jit(solution)/shard_map/ppermute | solution.py:17
  43.9 0.9 maximum_maximum_fusion
  44.8 0.0 copy-start.1
  44.8 0.4 copy.16
  45.3 0.6 copy-done.1
  45.8 17.2 %while.14 = (s32[]{:T(128)}, f32[64,32]{0,1:T(8,128)S(1)}, s32[64,2048]{1,0:T(8,128)S(1)}, bf16[2048,136]{0,1:T(8,128)(2,1)S(1)}, s32[]{:T(128)}, /*index=5*/s32...) while((s32[]{:T(128)}, f32[64,32]{0,1:T(8,128)S(1)}, ...), condition=%wide.region_3.4_spmd.clone, body=%wide.region_2.3_spmd.clone.sunk | while | flops 68161560 | bytes 3686781 | solution.py:92
  46.2 0.9 fusion.178
  47.6 0.9 fusion.178
  48.9 0.9 fusion.178
  50.2 0.9 fusion.178
  51.6 0.9 fusion.178
  52.9 0.9 fusion.178
  54.2 0.9 fusion.178
  55.5 0.9 fusion.178
  56.9 0.9 fusion.178
  58.2 0.9 fusion.178
  59.5 0.9 fusion.178
  60.9 0.9 fusion.178
  62.2 0.9 fusion.178
  63.1 35.0 %psum.14 = f32[64]{0:T(128)S(1)} all-reduce(f32[64]{0:T(128)S(1)} %get-tuple-element.123), channel_id=1, replica_groups=mesh['beam'=2,'tm'=16] {'tm'}, use_global_device_ids=true, to_apply=%region_5.6 | all-reduce | flops 64 | bytes 512 | tf_op jit(solution)/shard_map/psum | solution.py:118
  98.2 29.5 %psum.15 = f32[64]{0:T(128)S(1)} all-reduce(f32[64]{0:T(128)S(1)} %multiply_reduce_fusion.1), channel_id=1, replica_groups=mesh['beam'=2,'tm'=16] {'tm'}, use_global_device_ids=true, to_apply=%region_7.8 | all-reduce | flops 64 | bytes 512 | tf_op jit(solution)/shard_map/psum | solution.py:122
  127.7 29.5 %pmax.7 = f32[64]{0:T(128)S(1)} all-reduce(f32[64]{0:T(128)S(1)} %get-tuple-element.122), channel_id=1, replica_groups=mesh['beam'=2,'tm'=16] {'tm'}, use_global_device_ids=true, to_apply=%region_10.11 | all-reduce | flops 64 | bytes 512 | tf_op jit(solution)/shard_map/pmax | solution.py:119
  157.2 0.6 subtract_divide_fusion
  157.8 0.6 pad_maximum_fusion.2
  (128 shorter events, 4.2 us)
Async XLA Ops:
  2.0 5.2 %copy-start = (s32[2048]{0:T(1024)S(1)}, s32[2048]{0:T(1024)}, u32[]{:S(2)}) copy-start(s32[2048]{0:T(1024)} %param.7) | copy-start | bytes 24580
  2.2 5.8 %collective-permute-start = (bf16[2,2,15,2048]{3,2,0,1:T(8,128)(2,1)S(1)}, bf16[2,2,15,2048]{3,2,0,1:T(8,128)(2,1)S(1)}, u32[]{:S(2)}, u32[]{:S(2)}) collective-permute-start(bf16[2,2,15,2048]{3,2,0,1:T(8,128)(2,1)S(1)} %slice.217), channel_id=1, source_target_pairs={{0,1},{1,2},{2,3},{3,4},{4,5},{5,6},{6,7},{7,8},{8,9},{9,10},{10,1... | collective-permute-start | bytes 737288 | tf_op jit(solution)/shard_map/ppermute | solution.py:17
  17.4 5.9 %collective-permute-start.1 = (bf16[2048,32]{1,0:T(8,128)(2,1)S(1)}, bf16[2048,32]{1,0:T(8,128)(2,1)S(1)}, u32[]{:S(2)}, u32[]{:S(2)}) collective-permute-start(bf16[2048,32]{1,0:T(8,128)(2,1)S(1)} %bitcast_multiply_fusion), channel_id=1, source_target_pairs={{1,0},{2,1},{3,2},{4,3},{5,4},{6,5},{7,6},{8,7},{9,8},{10,9},{11,1... | collective-permute-start | bytes 393224 | tf_op jit(solution)/shard_map/ppermute | solution.py:17
  23.6 20.3 %collective-permute-start.2 = (bf16[2048,64]{1,0:T(8,128)(2,1)S(1)}, bf16[2048,64]{1,0:T(8,128)(2,1)S(1)}, u32[]{:S(2)}, u32[]{:S(2)}) collective-permute-start(bf16[2048,64]{1,0:T(8,128)(2,1)S(1)} %pad_maximum_fusion.1), channel_id=1, source_target_pairs={{2,0},{3,1},{4,2},{5,3},{6,4},{7,5},{8,6},{9,7},{10,8},{11,9},{12,... | collective-permute-start | bytes 786440 | tf_op jit(solution)/shard_map/ppermute | solution.py:17
  44.8 1.0 copy-start.1
where the time goes:
time: 159 us; the launch traced here: 158 us
  blocking collectives  94 us (59%)
  waiting for transfers between devices  22.7 us (14%)
  matrix products  17.3 us (11%)
  other arithmetic  8.09 us (5%)
  local copies, waits for them, and re-layouts  7.21 us (5%)
  starting transfers between devices  5.18 us (3%)
  between operations  2.24 us (1%)
  loops' own time  1.66 us (1%)
    psum x1, blocking collectives, per_device(): totals = lax.psum(jnp.sum(series, axis=1), 'tm')  35 us
    psum x1, blocking collectives, per_device(): variance = lax.psum(jnp.sum(centred * centred, axis=1), 'tm') / total_frames  29.5 us
    pmax x1, blocking collectives, per_device(): peak_value = lax.pmax(jnp.max(series, axis=1), 'tm')  29.5 us
    ppermute x3, waiting for transfers between devices, passed_along(): lax.ppermute(value, axis, [(source, source + steps) for source in range(f...  22.7 us
    dot_general x13, matrix products, add_group(): jnp.einsum('dsk,skt->dt', selector, stacked, preferred_element_type=jnp.f...  11.5 us
    ppermute x3, starting transfers between devices, passed_along(): lax.ppermute(value, axis, [(source, source + steps) for source in range(f...  5.18 us
    while x91, local copies, waits for them, and re-layouts  3.45 us
  transfers between devices with their start and end apart: 3, of which 2 were waited for; matrix products, arithmetic and copies ran while one was open for 2% of the time, Pallas kernels for 0%

commit v1 on v0

--- a/solution.py
+++ b/solution.py
@@ -119,7 +119,9 @@
     peak_value = lax.pmax(jnp.max(series, axis=1), "tm")
     average = totals / total_frames
     centred = series - average[:, None]
-    variance = lax.psum(jnp.sum(centred * centred, axis=1), "tm") / total_frames
+    variance = (
+        jnp.sum(lax.all_gather(jnp.sum(centred * centred, axis=1), "tm"), axis=0) / total_frames
+    )
     deviation = jnp.sqrt(variance + 1e-05)
     zscore = centred / deviation[:, None]
     live_count = jnp.maximum(jnp.sum(chan_mask).astype(jnp.float32), 1.0)

time: 159 us -> 159 us (level)
    psum x1 -> x0, blocking collectives: 29.5 us -> none  [per_device(): variance = lax.psum(jnp.sum(centred * centred, axis=1), 'tm') / total_frames]
    unnamed x0 -> x1, blocking collectives: none -> 29.5 us
where the time goes in v1:
time: 159 us
  blocking collectives  94 us (59%)
  waiting for transfers between devices  21.4 us (13%)
  matrix products  17.3 us (11%)
  local copies, waits for them, and re-layouts  8.13 us (5%)
  other arithmetic  8.11 us (5%)
  starting transfers between devices  5.18 us (3%)
  between operations  2.93 us (2%)
  loops' own time  1.66 us (1%)
    psum x1, blocking collectives, per_device(): totals = lax.psum(jnp.sum(series, axis=1), 'tm')  35 us
    pmax x1, blocking collectives, per_device(): peak_value = lax.pmax(jnp.max(series, axis=1), 'tm')  29.5 us
    unnamed x1, blocking collectives  29.5 us
    ppermute x3, waiting for transfers between devices, passed_along(): lax.ppermute(value, axis, [(source, source + steps) for source in range(f...  21.4 us
    dot_general x13, matrix products, add_group(): jnp.einsum('dsk,skt->dt', selector, stacked, preferred_element_type=jnp.f...  11.5 us
    ppermute x3, starting transfers between devices, passed_along(): lax.ppermute(value, axis, [(source, source + steps) for source in range(f...  5.18 us
    while x91, local copies, waits for them, and re-layouts  3.45 us
  transfers between devices with their start and end apart: 3, of which 2 were waited for; matrix products, arithmetic and copies ran while one was open for 2% of the time, Pallas kernels for 0%

profile of v1, /device:TPU:0, one launch (start us, length us, event | category | flops | bytes accessed | tf_op | source)
XLA Modules:
  0.0 158.7 jit_solution(12063745642957004767)
XLA Ops:
  0.6 1.4 reshape.133
  2.1 0.1 slice.217
  2.2 2.4 %collective-permute-start = (bf16[2,2,15,2048]{3,2,0,1:T(8,128)(2,1)S(1)}, bf16[2,2,15,2048]{3,2,0,1:T(8,128)(2,1)S(1)}, u32[]{:S(2)}, u32[]{:S(2)}) collective-permute-start(bf16[2,2,15,2048]{3,2,0,1:T(8,128)(2,1)S(1)} %slice.217), channel_id=1, source_target_pairs={{0,1},{1,2},{2,3},{3,4},{4,5},{5,6},{6,7},{7,8},{8,9},{9,10},{10,1... | collective-permute-start | bytes 737288 | tf_op jit(solution)/shard_map/ppermute | solution.py:17
  4.6 1.2 multiply_reduce_fusion
  6.6 0.6 broadcast_multiply_fusion
  7.2 0.6 fusion.155
  7.9 2.6 %multiply_add_fusion = f32[2,2,32,2048]{3,2,0,1:T(8,128)S(1)} fusion(bf16[2,2,32,2048]{3,2,0,1:T(8,128)(2,1)S(1)} %copy.17, bf16[2,2,15,2048]{3,2,0,1:T(8,128)(2,1)S(1)} %collective-permute-done, f32[2048]{0:T(1024)S(1)} %get-tuple-element.137, f32[2048]{0:T(1024)S(1)} %get-tuple-element.138, f32[2048]{0:T(1024)S(1)} %get-tuple-element.139, ...), kind=kLoop, calls=%fused_computation.61 | loop fusion | flops 24117248 | bytes 1949696 | tf_op jit(solution)/shard_map/add | solution.py:103
  10.6 0.2 copy.26
  10.8 0.6 fusion.45
  11.4 0.6 fusion.44
  12.0 0.6 convolution_subtract_fusion.1
  12.6 0.6 convolution_add_fusion.1
  13.2 0.8 fusion.40
  14.1 0.8 fusion.42
  14.9 0.8 fusion.22
  15.7 0.8 fusion.23
  16.6 0.5 copy.20
  17.1 0.3 bitcast_multiply_fusion
  17.4 1.3 collective-permute-start.1
  18.7 4.6 %collective-permute-done.1 = bf16[2048,32]{1,0:T(8,128)(2,1)S(1)} collective-permute-done((bf16[2048,32]{1,0:T(8,128)(2,1)S(1)}, bf16[2048,32]{1,0:T(8,128)(2,1)S(1)}, u32[]{:S(2)}, u32[]{:S(2)}) %collective-permute-start.1) | collective-permute-done | bytes 131104 | tf_op jit(solution)/shard_map/ppermute | solution.py:17
  23.3 0.3 pad_maximum_fusion.1
  23.6 1.5 collective-permute-start.2
  25.8 0.6 dynamic-slice
  27.0 16.8 %collective-permute-done.2 = bf16[2048,64]{1,0:T(8,128)(2,1)S(1)} collective-permute-done((bf16[2048,64]{1,0:T(8,128)(2,1)S(1)}, bf16[2048,64]{1,0:T(8,128)(2,1)S(1)}, u32[]{:S(2)}, u32[]{:S(2)}) %collective-permute-start.2) | collective-permute-done | bytes 262176 | tf_op jit(solution)/shard_map/ppermute | solution.py:17
  43.9 0.9 maximum_maximum_fusion
  44.8 0.4 copy.21
  45.3 0.6 copy-done.1
  45.9 17.2 %while.14 = (s32[]{:T(128)}, f32[64,32]{0,1:T(8,128)S(1)}, s32[64,2048]{1,0:T(8,128)S(1)}, bf16[2048,136]{0,1:T(8,128)(2,1)S(1)}, s32[]{:T(128)}, /*index=5*/s32...) while((s32[]{:T(128)}, f32[64,32]{0,1:T(8,128)S(1)}, ...), condition=%wide.region_3.4_spmd.clone, body=%wide.region_2.3_spmd.clone.sunk | while | flops 68161560 | bytes 3686781 | solution.py:92
  46.3 0.9 fusion.178
  47.6 0.9 fusion.178
  48.9 0.9 fusion.178
  50.2 0.9 fusion.178
  51.6 0.9 fusion.178
  52.9 0.9 fusion.178
  54.2 0.9 fusion.178
  55.6 0.9 fusion.178
  56.9 0.9 fusion.178
  58.2 0.9 fusion.178
  59.5 0.9 fusion.178
  60.9 0.9 fusion.178
  62.2 0.9 fusion.178
  63.1 35.0 %psum.7 = f32[64]{0:T(128)S(1)} all-reduce(f32[64]{0:T(128)S(1)} %get-tuple-element.127), channel_id=1, replica_groups=mesh['beam'=2,'tm'=16] {'tm'}, use_global_device_ids=true, to_apply=%region_5.6 | all-reduce | flops 64 | bytes 512 | tf_op jit(solution)/shard_map/psum | solution.py:118
  98.2 0.2 dynamic-update-slice
  98.4 29.5 %all-reduce = f32[1024]{0:T(1024)S(1)} all-reduce(f32[1024]{0:T(1024)S(1)} %dynamic-update-slice), channel_id=2, replica_groups=mesh['beam'=2,'tm'=16] {'tm'}, use_global_device_ids=true, to_apply=%add | all-reduce | flops 1024 | bytes 8192
  127.9 0.1 reshape.135
  128.0 29.5 %pmax.7 = f32[64]{0:T(128)S(1)} all-reduce(f32[64]{0:T(128)S(1)} %get-tuple-element.126), channel_id=1, replica_groups=mesh['beam'=2,'tm'=16] {'tm'}, use_global_device_ids=true, to_apply=%region_10.11 | all-reduce | flops 64 | bytes 512 | tf_op jit(solution)/shard_map/pmax | solution.py:119
  157.5 0.6 subtract_divide_fusion
  158.1 0.6 pad_maximum_fusion.2
  (135 shorter events, 4.3 us)
Async XLA Ops:
  2.0 5.2 %copy-start = (s32[2048]{0:T(1024)S(1)}, s32[2048]{0:T(1024)}, u32[]{:S(2)}) copy-start(s32[2048]{0:T(1024)} %param.7) | copy-start | bytes 24580
  2.2 5.8 %collective-permute-start = (bf16[2,2,15,2048]{3,2,0,1:T(8,128)(2,1)S(1)}, bf16[2,2,15,2048]{3,2,0,1:T(8,128)(2,1)S(1)}, u32[]{:S(2)}, u32[]{:S(2)}) collective-permute-start(bf16[2,2,15,2048]{3,2,0,1:T(8,128)(2,1)S(1)} %slice.217), channel_id=1, source_target_pairs={{0,1},{1,2},{2,3},{3,4},{4,5},{5,6},{6,7},{7,8},{8,9},{9,10},{10,1... | collective-permute-start | bytes 737288 | tf_op jit(solution)/shard_map/ppermute | solution.py:17
  17.4 8.4 %copy-start.2 = (u32[32]{0:T(128)S(1)}, u32[32]{0:T(128)}, u32[]{:S(2)}) copy-start(u32[32]{0:T(128)} %constant.151) | copy-start | bytes 388
  17.4 5.9 %collective-permute-start.1 = (bf16[2048,32]{1,0:T(8,128)(2,1)S(1)}, bf16[2048,32]{1,0:T(8,128)(2,1)S(1)}, u32[]{:S(2)}, u32[]{:S(2)}) collective-permute-start(bf16[2048,32]{1,0:T(8,128)(2,1)S(1)} %bitcast_multiply_fusion), channel_id=1, source_target_pairs={{1,0},{2,1},{3,2},{4,3},{5,4},{6,5},{7,6},{8,7},{9,8},{10,9},{11,1... | collective-permute-start | bytes 393224 | tf_op jit(solution)/shard_map/ppermute | solution.py:17
  23.6 20.3 %collective-permute-start.2 = (bf16[2048,64]{1,0:T(8,128)(2,1)S(1)}, bf16[2048,64]{1,0:T(8,128)(2,1)S(1)}, u32[]{:S(2)}, u32[]{:S(2)}) collective-permute-start(bf16[2048,64]{1,0:T(8,128)(2,1)S(1)} %pad_maximum_fusion.1), channel_id=1, source_target_pairs={{2,0},{3,1},{4,2},{5,3},{6,4},{7,5},{8,6},{9,7},{10,8},{11,9},{12,... | collective-permute-start | bytes 786440 | tf_op jit(solution)/shard_map/ppermute | solution.py:17
  44.8 1.0 copy-start.1
